TPU v7x, 32 devices: a whole 2x2x4 slice. The times are simulated.
32 devices in a mesh: expert: 8 (over y, x, core), replica: 4 (over z).
Axes of the slice: x: 2, y: 2, z: 4, core: 2. Of those that a mesh axis runs over, the one named last changes fastest.
Arguments:
- tokens_in: bfloat16 [8192, 2048], P(('expert', 'replica')), may hold values from -6 to 6
- cotangents: bfloat16 [8192, 8192], P(('expert', 'replica')), may hold values from -0.1796875 to 0.1796875
- left_root: bfloat16 [8, 2048, 2048], P('expert'), may hold values from -2 to 6, as said below
- right_root: bfloat16 [8, 8, 1024, 1024], P('expert', 'replica'), may hold values from -2 to 6, as said below
Outputs:
- update: bfloat16 [8, 2048, 8192], P('expert', None, 'replica')
Inputs may be any that keep to these rules, and one draw needn't show every extreme that they name: `left_root`: each matrix is symmetric. `right_root`: each block is symmetric.
All inputs are finite; a program needn't handle non-finite values.
Results may differ from a plain program's by a relative error of at most 0.0058.
Values may be sent and summed in bfloat16 or wider, within the bound.
A program may use at most 192 MiB of HBM per device.

v0:
```python
import jax
import jax.numpy as jnp
from jax import lax
from jax.sharding import PartitionSpec as P


def body(tokens_in, cotangents, left_root, right_root):
    expert_count = lax.axis_size("expert")
    replica_count = lax.axis_size("replica")
    local_experts = left_root.shape[0]
    width = left_root.shape[1]
    block_count = right_root.shape[1]
    block_size = right_root.shape[2]
    columns = cotangents.shape[1] // replica_count
    slot_count = tokens_in.shape[0] // (expert_count * local_experts)
    shaped = cotangents.reshape(1, expert_count, local_experts, slot_count, replica_count, columns)
    routed = lax.all_to_all(
        lax.all_to_all(shaped, "expert", split_axis=1, concat_axis=1, tiled=True),
        "replica",
        split_axis=4,
        concat_axis=0,
        tiled=True,
    )
    routed = routed.reshape(replica_count, expert_count, local_experts, slot_count, columns)
    tokens = tokens_in.reshape(expert_count, local_experts, slot_count, width)
    grouped = lax.all_to_all(tokens, "expert", split_axis=0, concat_axis=0, tiled=True)
    gradient = jnp.einsum(
        "rnxsd,rnxsf->xdf",
        lax.all_gather(grouped[None], "replica", axis=0, tiled=True),
        routed,
        preferred_element_type=jnp.float32,
    )
    gradient = gradient.astype(jnp.bfloat16)
    blocks = gradient.reshape(local_experts, width, block_count, block_size)
    applied = jnp.einsum("xdbk,xbkj->xdbj", blocks, right_root, preferred_element_type=jnp.float32)
    applied = applied.astype(jnp.bfloat16).reshape(local_experts, width, columns)
    update = jnp.einsum("xde,xef->xdf", left_root, applied, preferred_element_type=jnp.float32)
    return update.astype(jnp.bfloat16)


def solution(mesh):
    in_specs = (
        P(("expert", "replica"), None),
        P(("expert", "replica"), None),
        P("expert", None, None),
        P("expert", "replica", None, None),
    )
    out_specs = P("expert", None, "replica")
    return jax.shard_map(body, mesh=mesh, in_specs=in_specs, out_specs=out_specs, check_vma=False)
```

profile of v0, /device:TPU:0, one launch (start us, length us, event | category | flops | bytes accessed | tf_op | source)
XLA Modules:
  0.0 275.7 jit_solution(12691857189009747764)
XLA Ops:
  6.5 5.2 %all-to-all-start = ((bf16[8,1,32,2048]{3,2,1,0:T(8,128)(2,1)}), bf16[8,1,32,2048]{3,2,1,0:T(8,128)(2,1)S(1)}, u32[]{:S(2)}, u32[]{:S(2)}) async-start(bf16[8,1,32,2048]{3,2,1,0:T(8,128)(2,1)} %bitcast.41), calls=%async_computation | async-start | bytes 2097152 | tf_op jit(solution)/shard_map/all_to_all | solution.py:26
  11.7 7.8 %reshape.40 = bf16[1,8,1,32,4,2048]{5,4,3,1,2,0:T(4,128)(2,1)} reshape(bf16[256,8192]{1,0:T(8,128)(2,1)} %param.5) | data formatting | bytes 8388608 | tf_op jit(solution)/shard_map/reshape | solution.py:16
  19.5 6.6 %copy.13 = bf16[1,8,1,32,4,2048]{5,3,4,2,0,1:T(8,128)(2,1)} copy(bf16[1,8,1,32,4,2048]{5,4,3,1,2,0:T(4,128)(2,1)} %reshape.40) | data formatting | bytes 8388608 | tf_op jit(solution)/shard_map/reshape | solution.py:16
  26.1 1.0 all-to-all-done
  27.1 0.0 copy-start
  27.1 4.6 %all-to-all-start.1 = ((bf16[1,8,1,32,4,2048]{5,3,4,2,0,1:T(8,128)(2,1)}), bf16[1,8,1,32,4,2048]{5,3,4,2,0,1:T(8,128)(2,1)}, u32[]{:S(2)}, u32[]{:S(2)}) async-start(bf16[1,8,1,32,4,2048]{5,3,4,2,0,1:T(8,128)(2,1)} %copy.13), calls=%async_computation.1 | async-start | bytes 8388608 | tf_op jit(solution)/shard_map/all_to_all | solution.py:18
  31.7 0.0 all-gather.3.cloned.1.call-start
  31.8 0.0 copy-done
  31.8 0.7 all-gather.3.cloned.1.call-update
  32.4 48.4 %all-to-all-done.1 = bf16[1,8,1,32,4,2048]{5,3,4,2,0,1:T(8,128)(2,1)} async-done(((bf16[1,8,1,32,4,2048]{5,3,4,2,0,1:T(8,128)(2,1)}), bf16[1,8,1,32,4,2048]{5,3,4,2,0,1:T(8,128)(2,1)}, u32[]{:S(2)}, u32[]{:S(2)}) %all-to-all-start.1) | async-done | bytes 4194336 | tf_op jit(solution)/shard_map/all_to_all | solution.py:18
  80.8 4.8 %copy.14 = bf16[1,8,1,32,4,2048]{5,3,1,2,0,4:T(8,128)(2,1)} copy(bf16[1,8,1,32,4,2048]{5,3,4,2,0,1:T(8,128)(2,1)} %all-to-all-done.1) | data formatting | bytes 8388608 | tf_op jit(solution)/shard_map/all_to_all | solution.py:18
  85.6 5.0 %all-to-all-start.2 = ((bf16[1,8,1,32,4,2048]{5,3,1,2,0,4:T(8,128)(2,1)}), bf16[1,8,1,32,4,2048]{5,3,1,2,0,4:T(8,128)(2,1)}, u32[]{:S(2)}, u32[]{:S(2)}) async-start(bf16[1,8,1,32,4,2048]{5,3,1,2,0,4:T(8,128)(2,1)} %copy.14), calls=%async_computation.2 | async-start | bytes 8388608 | tf_op jit(solution)/shard_map/all_to_all | solution.py:17
  90.6 61.0 %all-gather.3.cloned.1.call-done = bf16[32,1,32,2048]{3,2,1,0:T(8,128)(2,1)} async-done(((bf16[8,1,32,2048]{3,2,1,0:T(8,128)(2,1)}), bf16[32,1,32,2048]{3,2,1,0:T(8,128)(2,1)}) %all-gather.3.cloned.1.call-update) | async-done | bytes 4194320 | tf_op jit(solution)/shard_map/all_gather | solution.py:29
  151.6 54.4 %all-to-all-done.2 = bf16[1,8,1,32,4,2048]{5,3,1,2,0,4:T(8,128)(2,1)} async-done(((bf16[1,8,1,32,4,2048]{5,3,1,2,0,4:T(8,128)(2,1)}), bf16[1,8,1,32,4,2048]{5,3,1,2,0,4:T(8,128)(2,1)}, u32[]{:S(2)}, u32[]{:S(2)}) %all-to-all-start.2) | async-done | bytes 4194336 | tf_op jit(solution)/shard_map/all_to_all | solution.py:17
  205.9 0.0 slice-start
  205.9 14.1 %bitcast_convert_fusion = bf16[2048,2048]{0,1:T(8,128)(2,1)} fusion(bf16[1,8,1,32,4,2048]{5,3,1,2,0,4:T(8,128)(2,1)} %all-to-all-done.2, bf16[4,8,32,2048]{3,2,1,0:T(8,128)(2,1)} %bitcast.44), kind=kOutput, calls=%fused_computation | convolution fusion | flops 8594128896 | bytes 16777216 | tf_op jit(solution)/shard_map/rnxsd,rnxsf->xdf/dot_general | solution.py:27
  220.1 0.0 slice-start.1
  220.1 14.8 %convolution_convert_fusion = bf16[2,2048,1024]{1,2,0:T(8,128)(2,1)} fusion(bf16[2048,2,1024]{0,2,1:T(8,128)(2,1)} %bitcast.45, bf16[1,2,1024,1024]{3,2,1,0:T(8,128)(2,1)} %param.7), kind=kOutput, calls=%fused_computation.4 | convolution fusion | flops 8594128896 | bytes 20971520 | tf_op jit(solution)/shard_map/xdbk,xbkj->xdbj/dot_general | solution.py:35
  234.9 0.0 slice-done
  234.9 0.0 slice-done.1
  234.9 21.8 %convert_bitcast_fusion = bf16[1,2048,2048]{1,2,0:T(8,128)(2,1)} fusion(bf16[2048,2048]{0,1:T(8,128)(2,1)} %bitcast.46, bf16[1,2048,2048]{2,1,0:T(8,128)(2,1)S(1)} %bitcast.43), kind=kOutput, calls=%fused_computation.3 | convolution fusion | flops 17184063488 | bytes 25165824 | tf_op jit(solution)/shard_map/xde,xef->xdf/dot_general | solution.py:37
  256.7 12.2 %copy.19 = bf16[1,2048,2048]{2,1,0:T(8,128)(2,1)} copy(bf16[1,2048,2048]{1,2,0:T(8,128)(2,1)} %convert_bitcast_fusion) | data formatting | bytes 16777216 | tf_op jit(solution)/shard_map/convert_element_type | solution.py:38
  (1 shorter events, 0.0 us)
Async XLA Ops:
  6.5 20.6 %all-to-all-start = ((bf16[8,1,32,2048]{3,2,1,0:T(8,128)(2,1)}), bf16[8,1,32,2048]{3,2,1,0:T(8,128)(2,1)S(1)}, u32[]{:S(2)}, u32[]{:S(2)}) async-start(bf16[8,1,32,2048]{3,2,1,0:T(8,128)(2,1)} %bitcast.41), calls=%async_computation | async-start | bytes 2097152 | tf_op jit(solution)/shard_map/all_to_all | solution.py:26
  27.1 4.6 %copy-start = (bf16[8,1,32,2048]{3,2,1,0:T(8,128)(2,1)}, bf16[8,1,32,2048]{3,2,1,0:T(8,128)(2,1)S(1)}, u32[]{:S(2)}) copy-start(bf16[8,1,32,2048]{3,2,1,0:T(8,128)(2,1)S(1)} %all-to-all-done) | copy-start | bytes 3145732
  27.1 53.7 %all-to-all-start.1 = ((bf16[1,8,1,32,4,2048]{5,3,4,2,0,1:T(8,128)(2,1)}), bf16[1,8,1,32,4,2048]{5,3,4,2,0,1:T(8,128)(2,1)}, u32[]{:S(2)}, u32[]{:S(2)}) async-start(bf16[1,8,1,32,4,2048]{5,3,4,2,0,1:T(8,128)(2,1)} %copy.13), calls=%async_computation.1 | async-start | bytes 8388608 | tf_op jit(solution)/shard_map/all_to_all | solution.py:18
  31.7 119.9 %all-gather.3.cloned.1.call-start = ((), (), s32[]{:S(2)}) async-start(), calls=%async_computation.3 | async-start | bytes 5242880 | tf_op jit(solution)/shard_map/all_gather | solution.py:29
  85.6 120.3 %all-to-all-start.2 = ((bf16[1,8,1,32,4,2048]{5,3,1,2,0,4:T(8,128)(2,1)}), bf16[1,8,1,32,4,2048]{5,3,1,2,0,4:T(8,128)(2,1)}, u32[]{:S(2)}, u32[]{:S(2)}) async-start(bf16[1,8,1,32,4,2048]{5,3,1,2,0,4:T(8,128)(2,1)} %copy.14), calls=%async_computation.2 | async-start | bytes 8388608 | tf_op jit(solution)/shard_map/all_to_all | solution.py:17
  205.9 28.9 %slice-start = ((s8[8388608]{0:T(1024)(128)(4,1)}), s8[4194304]{0:T(1024)(128)(4,1)S(1)}, s32[]{:S(2)}) async-start(s8[8388608]{0:T(1024)(128)(4,1)} %bitcast.42), calls=%async_computation.4 | async-start | bytes 8388608
  220.1 14.8 %slice-start.1 = ((s8[8388608]{0:T(1024)(128)(4,1)}), s8[4194304]{0:T(1024)(128)(4,1)S(1)}, s32[]{:S(2)}) async-start(s8[8388608]{0:T(1024)(128)(4,1)} %bitcast.42), calls=%async_computation.5 | async-start | bytes 8388608
Sparse Core Ops, SparseCore 0:
  34.1 117.4 all-gather.2
where the time goes:
time: 277 us; the launch traced here: 276 us
  waiting for transfers between devices  165 us (60%)
  matrix products  50.7 us (18%)
  local copies, waits for them, and re-layouts  31.4 us (11%)
  starting transfers between devices  14.8 us (5%)
  between operations  13.4 us (5%)
    all_gather x1, waiting for transfers between devices, body(): lax.all_gather(grouped[None], 'replica', axis=0, tiled=True)  61 us
    all_to_all x1, waiting for transfers between devices, body(): lax.all_to_all(lax.all_to_all(shaped, 'expert', split_axis=1, concat_axis...  54.4 us
    all_to_all x1, waiting for transfers between devices, body(): lax.all_to_all(shaped, 'expert', split_axis=1, concat_axis=1, tiled=True)  48.4 us
    dot_general x1, matrix products, body(): jnp.einsum('xde,xef->xdf', left_root, applied, preferred_element_type=jnp...  21.8 us
    dot_general x1, matrix products, body(): jnp.einsum('xdbk,xbkj->xdbj', blocks, right_root, preferred_element_type=...  14.8 us
    reshape x2, local copies, waits for them, and re-layouts, body(): cotangents.reshape(1, expert_count, local_experts, slot_count, replica_co...  14.4 us
    dot_general x1, matrix products, body(): jnp.einsum('rnxsd,rnxsf->xdf', lax.all_gather(grouped[None], 'replica', a...  14.1 us
    convert_element_type x1, local copies, waits for them, and re-layouts, body(): return update.astype(jnp.bfloat16)  12.2 us
  transfers between devices with their start and end apart: 4, of which 4 were waited for; matrix products, arithmetic and copies ran while one was open for 7% of the time, Pallas kernels for 0%

commit v1 on v0

--- a/solution.py
+++ b/solution.py
@@ -5,6 +5,18 @@
 
 
 def body(tokens_in, cotangents, left_root, right_root):
+
+    def launch_forms(s0, comm_axis, message):
+        m_next, known, heard = (lax.axis_size(comm_axis), lax.axis_index(comm_axis), s0.shape[0])
+        series = [(j, (j + 1) % m_next) for j in range(m_next)]
+        taken_in, front = (s0, None)
+        for w in range(m_next):
+            kept_arr = lax.ppermute(taken_in, comm_axis, series) if w < m_next - 1 else None
+            y1 = message(taken_in, (known - w) % m_next * heard)
+            front = y1 if front is None else front + y1
+            taken_in = kept_arr
+        return front
+
     expert_count = lax.axis_size("expert")
     replica_count = lax.axis_size("replica")
     local_experts = left_root.shape[0]
@@ -24,11 +36,15 @@
     routed = routed.reshape(replica_count, expert_count, local_experts, slot_count, columns)
     tokens = tokens_in.reshape(expert_count, local_experts, slot_count, width)
     grouped = lax.all_to_all(tokens, "expert", split_axis=0, concat_axis=0, tiled=True)
-    gradient = jnp.einsum(
-        "rnxsd,rnxsf->xdf",
-        lax.all_gather(grouped[None], "replica", axis=0, tiled=True),
-        routed,
-        preferred_element_type=jnp.float32,
+    gradient = launch_forms(
+        grouped[None],
+        "replica",
+        lambda own_block, start: jnp.einsum(
+            "rnxsd,rnxsf->xdf",
+            own_block,
+            lax.dynamic_slice_in_dim(routed, start, own_block.shape[0], axis=0),
+            preferred_element_type=jnp.float32,
+        ),
     )
     gradient = gradient.astype(jnp.bfloat16)
     blocks = gradient.reshape(local_experts, width, block_count, block_size)

time: 277 us -> 347 us (1.25)
  blocking collectives: 0 us -> 54.1 us
  matrix products: 50.7 us -> 85.4 us
  waiting for transfers between devices: 165 us -> 140 us
  starting transfers between devices: 14.8 us -> 36.8 us
  between operations: 13.4 us -> 0.03 us
    ppermute x0 -> x3, waiting for transfers between devices: none -> 108 us  [launch_forms(): lax.ppermute(taken_in, comm_axis, series)]
    all_gather x1 -> x0, waiting for transfers between devices: 61 us -> none  [body(): lax.all_gather(grouped[None], 'replica', axis=0, tiled=True)]
    all_to_all x0 -> x1, blocking collectives: none -> 54.1 us  [body(): lax.all_to_all(shaped, 'expert', split_axis=1, concat_axis=1, tiled=True)]
    all_to_all x1 -> x0, waiting for transfers between devices: 48.4 us -> none  [body(): lax.all_to_all(shaped, 'expert', split_axis=1, concat_axis=1, tiled=True)]
    dot_general x1 -> x4, matrix products: 14.1 us -> 49.2 us  [body(): jnp.einsum('rnxsd,rnxsf->xdf', own_block, lax.dynamic_slice_in_dim(routed...]
    all_to_all x1, waiting for transfers between devices: 54.4 us -> 21.8 us  [body(): lax.all_to_all(lax.all_to_all(shaped, 'expert', split_axis=1, concat_axis...]
    ppermute x0 -> x3, starting transfers between devices: none -> 28.4 us  [launch_forms(): lax.ppermute(taken_in, comm_axis, series)]
    all_to_all x1, waiting for transfers between devices: 1 us -> 10.5 us  [body(): lax.all_to_all(tokens, 'expert', split_axis=0, concat_axis=0, tiled=True)]
  transfers between devices with their start and end apart: 4 -> 5, of which waited for: 4 -> 4; matrix products, arithmetic and copies ran while one was open for 7% -> 10% of each run, Pallas kernels for 0% -> 0%
where the time goes in v1:
time: 347 us; the launch traced here: 346 us
  waiting for transfers between devices  140 us (40%)
  matrix products  85.4 us (25%)
  blocking collectives  54.1 us (16%)
  starting transfers between devices  36.8 us (11%)
  local copies, waits for them, and re-layouts  29.4 us (8%)
    ppermute x3, waiting for transfers between devices, launch_forms(): lax.ppermute(taken_in, comm_axis, series)  108 us
    all_to_all x1, blocking collectives, body(): lax.all_to_all(shaped, 'expert', split_axis=1, concat_axis=1, tiled=True)  54.1 us
    dot_general x4, matrix products, body(): jnp.einsum('rnxsd,rnxsf->xdf', own_block, lax.dynamic_slice_in_dim(routed...  49.2 us
    ppermute x3, starting transfers between devices, launch_forms(): lax.ppermute(taken_in, comm_axis, series)  28.4 us
    all_to_all x1, waiting for transfers between devices, body(): lax.all_to_all(lax.all_to_all(shaped, 'expert', split_axis=1, concat_axis...  21.8 us
    dot_general x1, matrix products, body(): jnp.einsum('xde,xef->xdf', left_root, applied, preferred_element_type=jnp...  21.6 us
    dot_general x1, matrix products, body(): jnp.einsum('xdbk,xbkj->xdbj', blocks, right_root, preferred_element_type=...  14.6 us
    reshape x2, local copies, waits for them, and re-layouts, body(): cotangents.reshape(1, expert_count, local_experts, slot_count, replica_co...  12.4 us
  transfers between devices with their start and end apart: 5, of which 4 were waited for; matrix products, arithmetic and copies ran while one was open for 10% of the time, Pallas kernels for 0%

profile of v1, /device:TPU:0, one launch (start us, length us, event | category | flops | bytes accessed | tf_op | source)
XLA Modules:
  0.0 346.0 jit_solution(11676960317589416908)
XLA Ops:
  0.0 7.8 %reshape.86 = bf16[1,8,1,32,4,2048]{5,4,3,1,2,0:T(4,128)(2,1)} reshape(bf16[256,8192]{1,0:T(8,128)(2,1)} %param.5) | data formatting | bytes 8388608 | tf_op jit(solution)/shard_map/reshape | solution.py:28
  7.8 4.6 %copy.13 = bf16[1,8,1,32,4,2048]{5,3,4,2,0,1:T(8,128)(2,1)S(1)} copy(bf16[1,8,1,32,4,2048]{5,4,3,1,2,0:T(4,128)(2,1)} %reshape.86) | data formatting | bytes 8388608 | tf_op jit(solution)/shard_map/reshape | solution.py:28
  12.4 54.1 %all_to_all.19 = bf16[1,8,1,32,4,2048]{5,3,4,2,0,1:T(8,128)(2,1)} all-to-all(bf16[1,8,1,32,4,2048]{5,3,4,2,0,1:T(8,128)(2,1)S(1)} %copy.13), channel_id=1, replica_groups=mesh['expert'=8,'replica'=4] {'expert'}, dimensions={1} | all-to-all | bytes 8388608 | tf_op jit(solution)/shard_map/all_to_all | solution.py:30
  66.5 3.6 %all-to-all-start.2 = ((bf16[8,1,32,2048]{3,2,1,0:T(8,128)(2,1)}), bf16[8,1,32,2048]{3,2,1,0:T(8,128)(2,1)S(1)}, u32[]{:S(2)}, u32[]{:S(2)}) async-start(bf16[8,1,32,2048]{3,2,1,0:T(8,128)(2,1)} %bitcast.1), calls=%async_computation.2 | async-start | bytes 2097152 | tf_op jit(solution)/shard_map/all_to_all | solution.py:38
  70.1 4.8 %copy.14 = bf16[1,8,1,32,4,2048]{5,3,1,2,0,4:T(8,128)(2,1)} copy(bf16[1,8,1,32,4,2048]{5,3,4,2,0,1:T(8,128)(2,1)} %all_to_all.19) | data formatting | bytes 8388608 | tf_op jit(solution)/shard_map/all_to_all | solution.py:30
  74.9 10.5 %all-to-all-done.2 = bf16[8,1,32,2048]{3,2,1,0:T(8,128)(2,1)S(1)} async-done(((bf16[8,1,32,2048]{3,2,1,0:T(8,128)(2,1)}), bf16[8,1,32,2048]{3,2,1,0:T(8,128)(2,1)S(1)}, u32[]{:S(2)}, u32[]{:S(2)}) %all-to-all-start.2) | async-done | bytes 1048608 | tf_op jit(solution)/shard_map/all_to_all | solution.py:38
  85.4 4.9 %all-to-all-start.1 = ((bf16[1,8,1,32,4,2048]{5,3,1,2,0,4:T(8,128)(2,1)}), bf16[1,8,1,32,4,2048]{5,3,1,2,0,4:T(8,128)(2,1)}, u32[]{:S(2)}, u32[]{:S(2)}) async-start(bf16[1,8,1,32,4,2048]{5,3,1,2,0,4:T(8,128)(2,1)} %copy.14), calls=%async_computation.1 | async-start | bytes 8388608 | tf_op jit(solution)/shard_map/all_to_all | solution.py:29
  90.3 2.0 collective-permute-start
  92.3 89.7 %collective-permute-done = bf16[1,8,1,32,2048]{4,3,1,2,0:T(8,128)(2,1)S(1)} collective-permute-done((bf16[1,8,1,32,2048]{4,3,1,2,0:T(8,128)(2,1)S(1)}, bf16[1,8,1,32,2048]{4,3,1,2,0:T(8,128)(2,1)S(1)}, u32[]{:S(2)}, u32[]{:S(2)}) %collective-permute-start) | collective-permute-done | bytes 1048608 | tf_op jit(solution)/shard_map/ppermute | solution.py:14
  182.0 21.3 %collective-permute-start.1 = (bf16[1,8,1,32,2048]{4,3,1,2,0:T(8,128)(2,1)S(1)}, bf16[1,8,1,32,2048]{4,3,1,2,0:T(8,128)(2,1)S(1)}, u32[]{:S(2)}, u32[]{:S(2)}) collective-permute-start(bf16[1,8,1,32,2048]{4,3,1,2,0:T(8,128)(2,1)S(1)} %collective-permute-done), channel_id=1, source_target_pairs={{0,1},{1,2},{2,3},{3,0},{4,5},{5,6},{6,7},{7,4},{8,9},{9,10},{10,1... | collective-permute-start | bytes 3145736 | tf_op jit(solution)/shard_map/ppermute | solution.py:14
  203.3 18.2 %collective-permute-done.1 = bf16[1,8,1,32,2048]{4,3,1,2,0:T(8,128)(2,1)S(1)} collective-permute-done((bf16[1,8,1,32,2048]{4,3,1,2,0:T(8,128)(2,1)S(1)}, bf16[1,8,1,32,2048]{4,3,1,2,0:T(8,128)(2,1)S(1)}, u32[]{:S(2)}, u32[]{:S(2)}) %collective-permute-start.1) | collective-permute-done | bytes 1048608 | tf_op jit(solution)/shard_map/ppermute | solution.py:14
  221.5 5.1 %collective-permute-start.2 = (bf16[1,8,1,32,2048]{4,3,1,2,0:T(8,128)(2,1)S(1)}, bf16[1,8,1,32,2048]{4,3,1,2,0:T(8,128)(2,1)}, u32[]{:S(2)}, u32[]{:S(2)}) collective-permute-start(bf16[1,8,1,32,2048]{4,3,1,2,0:T(8,128)(2,1)S(1)} %collective-permute-done.1), channel_id=1, source_target_pairs={{0,1},{1,2},{2,3},{3,0},{4,5},{5,6},{6,7},{7,4},{8,9},{9,10},{10,1... | collective-permute-start | bytes 3145736 | tf_op jit(solution)/shard_map/ppermute | solution.py:14
  226.6 21.8 %all-to-all-done.1 = bf16[1,8,1,32,4,2048]{5,3,1,2,0,4:T(8,128)(2,1)} async-done(((bf16[1,8,1,32,4,2048]{5,3,1,2,0,4:T(8,128)(2,1)}), bf16[1,8,1,32,4,2048]{5,3,1,2,0,4:T(8,128)(2,1)}, u32[]{:S(2)}, u32[]{:S(2)}) %all-to-all-start.1) | async-done | bytes 4194336 | tf_op jit(solution)/shard_map/all_to_all | solution.py:29
  248.3 9.3 %fusion.8 = f32[2048,2048,1]{1,0,2:T(8,128)} fusion(bf16[1,8,1,32,2048]{4,3,1,2,0:T(8,128)(2,1)S(1)} %collective-permute-done.1, bf16[1,8,1,32,4,2048]{5,3,1,2,0,4:T(8,128)(2,1)} %all-to-all-done.1, s32[]{:T(128)S(6)} %select_n.36), kind=kOutput, calls=%fused_computation.11 | convolution fusion | flops 2147483648 | bytes 18874372 | tf_op jit(solution)/shard_map/rnxsd,rnxsf->xdf/dot_general | solution.py:42
  257.7 9.3 %fusion.11 = f32[2048,2048,1]{1,0,2:T(8,128)} fusion(bf16[1,8,1,32,2048]{4,3,1,2,0:T(8,128)(2,1)S(1)} %collective-permute-done, bf16[1,8,1,32,4,2048]{5,3,1,2,0,4:T(8,128)(2,1)} %all-to-all-done.1, s32[]{:T(128)S(6)} %select_n.34), kind=kOutput, calls=%fused_computation.14 | convolution fusion | flops 2147483648 | bytes 18874372 | tf_op jit(solution)/shard_map/rnxsd,rnxsf->xdf/dot_general | solution.py:42
  267.0 0.0 slice-start
  267.0 9.5 %fusion.14 = f32[2048,2048,1]{1,0,2:T(8,128)} fusion(bf16[8,1,32,2048]{3,2,1,0:T(8,128)(2,1)S(1)} %all-to-all-done.2, bf16[1,8,1,32,4,2048]{5,3,1,2,0,4:T(8,128)(2,1)} %all-to-all-done.1, s32[]{:T(128)S(6)} %select_n.32), kind=kOutput, calls=%fused_computation.17 | convolution fusion | flops 2147483648 | bytes 18874372 | tf_op jit(solution)/shard_map/rnxsd,rnxsf->xdf/dot_general | solution.py:42
  276.5 0.0 slice-start.1
  276.5 0.0 collective-permute-done.2
  276.5 21.1 %fusion = bf16[2048,2048]{1,0:T(8,128)(2,1)} fusion(f32[2048,2048,1]{1,0,2:T(8,128)} %fusion.8, f32[2048,2048,1]{1,0,2:T(8,128)} %fusion.11, f32[2048,2048,1]{1,0,2:T(8,128)} %fusion.14, bf16[1,8,1,32,2048]{4,3,1,2,0:T(8,128)(2,1)} %collective-permute-done.2, bf16[1,8,1,32,4,2048]{5,3,1,2,0,4:T(8,128)(2,1)} %all-to-all-done.1, s32[]{:T(128)S(6)} %select_n.38), kind=kOutput, calls=%fused_computation.1 | convolution fusion | flops 2164260864 | bytes 60817412 | tf_op jit(solution)/shard_map/rnxsd,rnxsf->xdf/dot_general | solution.py:42
  297.6 14.6 %convolution_convert_fusion = bf16[2,2048,1024]{1,2,0:T(8,128)(2,1)} fusion(bf16[2048,2,1024]{0,2,1:T(8,128)(2,1)} %bitcast.67, bf16[1,2,1024,1024]{3,2,1,0:T(8,128)(2,1)} %param.7), kind=kOutput, calls=%fused_computation.7 | convolution fusion | flops 8594128896 | bytes 20971520 | tf_op jit(solution)/shard_map/xdbk,xbkj->xdbj/dot_general | solution.py:51
  312.2 0.0 slice-done
  312.2 0.0 slice-done.1
  312.2 21.6 %convert_bitcast_fusion = bf16[1,2048,2048]{1,2,0:T(8,128)(2,1)} fusion(bf16[2048,2048]{0,1:T(8,128)(2,1)} %bitcast.68, bf16[1,2048,2048]{2,1,0:T(8,128)(2,1)S(1)} %bitcast.66), kind=kOutput, calls=%fused_computation.6 | convolution fusion | flops 17184063488 | bytes 25165824 | tf_op jit(solution)/shard_map/xde,xef->xdf/dot_general | solution.py:53
  333.7 12.2 %copy.17 = bf16[1,2048,2048]{2,1,0:T(8,128)(2,1)} copy(bf16[1,2048,2048]{1,2,0:T(8,128)(2,1)} %convert_bitcast_fusion) | data formatting | bytes 16777216 | tf_op jit(solution)/shard_map/convert_element_type | solution.py:54
  (1 shorter events, 0.0 us)
Async XLA Ops:
  66.5 18.9 %all-to-all-start.2 = ((bf16[8,1,32,2048]{3,2,1,0:T(8,128)(2,1)}), bf16[8,1,32,2048]{3,2,1,0:T(8,128)(2,1)S(1)}, u32[]{:S(2)}, u32[]{:S(2)}) async-start(bf16[8,1,32,2048]{3,2,1,0:T(8,128)(2,1)} %bitcast.1), calls=%async_computation.2 | async-start | bytes 2097152 | tf_op jit(solution)/shard_map/all_to_all | solution.py:38
  85.4 162.9 %all-to-all-start.1 = ((bf16[1,8,1,32,4,2048]{5,3,1,2,0,4:T(8,128)(2,1)}), bf16[1,8,1,32,4,2048]{5,3,1,2,0,4:T(8,128)(2,1)}, u32[]{:S(2)}, u32[]{:S(2)}) async-start(bf16[1,8,1,32,4,2048]{5,3,1,2,0,4:T(8,128)(2,1)} %copy.14), calls=%async_computation.1 | async-start | bytes 8388608 | tf_op jit(solution)/shard_map/all_to_all | solution.py:29
  90.3 91.7 %collective-permute-start = (bf16[1,8,1,32,2048]{4,3,1,2,0:T(8,128)(2,1)S(1)}, bf16[1,8,1,32,2048]{4,3,1,2,0:T(8,128)(2,1)S(1)}, u32[]{:S(2)}, u32[]{:S(2)}) collective-permute-start(bf16[1,8,1,32,2048]{4,3,1,2,0:T(8,128)(2,1)S(1)} %bitcast.64), channel_id=1, source_target_pairs={{0,1},{1,2},{2,3},{3,0},{4,5},{5,6},{6,7},{7,4},{8,9},{9,10},{10,1... | collective-permute-start | bytes 3145736 | tf_op jit(solution)/shard_map/ppermute | solution.py:14
  182.0 39.5 %collective-permute-start.1 = (bf16[1,8,1,32,2048]{4,3,1,2,0:T(8,128)(2,1)S(1)}, bf16[1,8,1,32,2048]{4,3,1,2,0:T(8,128)(2,1)S(1)}, u32[]{:S(2)}, u32[]{:S(2)}) collective-permute-start(bf16[1,8,1,32,2048]{4,3,1,2,0:T(8,128)(2,1)S(1)} %collective-permute-done), channel_id=1, source_target_pairs={{0,1},{1,2},{2,3},{3,0},{4,5},{5,6},{6,7},{7,4},{8,9},{9,10},{10,1... | collective-permute-start | bytes 3145736 | tf_op jit(solution)/shard_map/ppermute | solution.py:14
  221.5 55.0 %collective-permute-start.2 = (bf16[1,8,1,32,2048]{4,3,1,2,0:T(8,128)(2,1)S(1)}, bf16[1,8,1,32,2048]{4,3,1,2,0:T(8,128)(2,1)}, u32[]{:S(2)}, u32[]{:S(2)}) collective-permute-start(bf16[1,8,1,32,2048]{4,3,1,2,0:T(8,128)(2,1)S(1)} %collective-permute-done.1), channel_id=1, source_target_pairs={{0,1},{1,2},{2,3},{3,0},{4,5},{5,6},{6,7},{7,4},{8,9},{9,10},{10,1... | collective-permute-start | bytes 3145736 | tf_op jit(solution)/shard_map/ppermute | solution.py:14
  267.0 45.2 %slice-start = ((s8[8388608]{0:T(1024)(128)(4,1)}), s8[4194304]{0:T(1024)(128)(4,1)S(1)}, s32[]{:S(2)}) async-start(s8[8388608]{0:T(1024)(128)(4,1)} %bitcast.65), calls=%async_computation.3 | async-start | bytes 8388608
  276.5 35.7 %slice-start.1 = ((s8[8388608]{0:T(1024)(128)(4,1)}), s8[4194304]{0:T(1024)(128)(4,1)S(1)}, s32[]{:S(2)}) async-start(s8[8388608]{0:T(1024)(128)(4,1)} %bitcast.65), calls=%async_computation.4 | async-start | bytes 8388608
